TPU v7x, 256 devices: a whole 4x4x8 slice. The times are simulated.
256 devices in a mesh: rep: 8 (over x_lo, y), tp: 8 (over z), fs: 4 (over x_hi, core).
Axes of the slice: x: 4 (x_hi: 2, x_lo: 2; x = x_hi * 2 + x_lo), y: 4, z: 8, core: 2. Of those that a mesh axis runs over, the one named last changes fastest.
Arguments:
- hidden: bfloat16 [64, 8192], P(('rep', 'fs'), 'tp'), may hold values from -6 to 6
- cache_key: bfloat16 [64, 2048, 1024], P(('rep', 'fs'), None, 'tp'), may hold values from -1300 to 1300
- cache_value: bfloat16 [64, 2048, 1024], P(('rep', 'fs'), None, 'tp'), may hold values from -6 to 6
- lengths: int32 [64], P(('rep', 'fs')), may hold values from 8 to 2047
- owner: int32 [1], replicated, may hold values from 0 to 32767
- query_weight: bfloat16 [8, 8192, 4096], P('rep', 'fs', 'tp'), may hold values from -0.0625 to 0.0625
- key_weight: bfloat16 [8, 8192, 1024], P('rep', 'fs', 'tp'), may hold values from -0.0625 to 0.0625
- value_weight: bfloat16 [8, 8192, 1024], P('rep', 'fs', 'tp'), may hold values from -0.0625 to 0.0625
- out_weight: bfloat16 [8, 4096, 8192], P('rep', 'tp', 'fs'), may hold values from -0.09375 to 0.09375
Outputs:
- mixed: bfloat16 [64, 8192], P(('rep', 'fs'), 'tp')
- new_key: bfloat16 [64, 1024], P(('rep', 'fs'), 'tp')
- new_value: bfloat16 [64, 1024], P(('rep', 'fs'), 'tp')
- fresh_query: bfloat16 [8, 8192, 4096], P('rep', 'fs', 'tp')
- fresh_key: bfloat16 [8, 8192, 1024], P('rep', 'fs', 'tp')
- fresh_value: bfloat16 [8, 8192, 1024], P('rep', 'fs', 'tp')
- fresh_out: bfloat16 [8, 4096, 8192], P('rep', 'tp', 'fs')
Inputs may be any that keep to these rules, and one draw needn't show every extreme that they name: `lengths`: the number of positions already in each sequence's cache; the new token stands at that position.
All inputs are finite; a program needn't handle non-finite values.
Results may differ from a plain program's by a relative error of at most 0.0065.
Values may be sent and summed in bfloat16 or wider, within the bound.
No kernel may reach another device: no remote copies, remote signals or barrier semaphores. Data moves between devices by JAX's collectives and lax.ppermute only.
A program may use at most 64 MiB of HBM per device.

v0:
```python
import jax
import jax.numpy as jnp
from jax import lax
from jax.sharding import PartitionSpec as P

DH = 128
rope_base = 500000.0
epsilon = 1e-05


def from_root(shard, axis, root):
    mine = lax.axis_index(axis) == root
    return lax.psum(jnp.where(mine, shard, jnp.zeros_like(shard)), axis)


def cut_along(shard, dim, peers):
    lengths = shard.shape
    parts = shard.reshape(*lengths[:dim], peers, lengths[dim] // peers, *lengths[dim + 1 :])
    return jnp.moveaxis(parts, dim, 0)


def sent_and_summed(shard, axis, dim):
    peers = lax.axis_size(axis)
    parts = lax.all_to_all(cut_along(shard, dim, peers), axis, 0, 0, tiled=True)
    return jnp.sum(parts, axis=0)


def copy_for_each(shard, axis):
    peers = lax.axis_size(axis)
    return lax.all_to_all(
        jnp.broadcast_to(shard[None], (peers, *shard.shape)), axis, 0, 0, tiled=True
    )


def joined_along(parts, dim):
    parts = jnp.moveaxis(parts, 0, dim)
    lengths = parts.shape
    return parts.reshape(*lengths[:dim], lengths[dim] * lengths[dim + 1], *lengths[dim + 2 :])


def collect(shard, axis, dim):
    parts = copy_for_each(shard, axis)
    return joined_along(parts, dim)


def rotate(heads, positions):
    half_dim = heads.shape[-1] // 2
    frequency = rope_base ** (-(jnp.arange(half_dim, dtype=jnp.float32) * 2.0 / heads.shape[-1]))
    angles = positions.astype(jnp.float32)[:, None] * frequency[None, :]
    cosine = jnp.cos(angles)[:, None, :]
    sine_part = jnp.sin(angles)[:, None, :]
    first_half = heads[..., :half_dim]
    second_half = heads[..., half_dim:]
    return jnp.concatenate(
        [
            first_half * cosine - second_half * sine_part,
            second_half * cosine + first_half * sine_part,
        ],
        axis=-1,
    )


def attend(query, own_key, own_value, cache_key, cache_value, lengths):
    seqs, span, width = cache_key.shape
    kv_local = query.shape[1]
    head_size = query.shape[3]
    keys_view = cache_key.reshape(seqs, span, kv_local, head_size)
    values_view = cache_value.reshape(seqs, span, kv_local, head_size)
    scale = head_size ** (-0.5)
    scores = (
        jnp.einsum("shgd,sthd->shgt", query, keys_view, preferred_element_type=jnp.float32) * scale
    )
    own_score = (
        jnp.einsum("shgd,shd->shg", query, own_key, preferred_element_type=jnp.float32) * scale
    )
    live = (jnp.arange(span, dtype=jnp.int32)[None, :] < lengths[:, None])[:, None, None, :]
    masked = jnp.where(live, scores, -jnp.inf)
    row_max = jnp.maximum(jnp.max(masked, axis=-1), own_score)
    weights = jnp.where(live, jnp.exp(scores - row_max[..., None]), 0.0)
    own_weight = jnp.exp(own_score - row_max)
    denominator = jnp.sum(weights, axis=-1) + own_weight
    probs = (weights / denominator[..., None]).astype(jnp.bfloat16)
    own_prob = (own_weight / denominator).astype(jnp.bfloat16)
    context = jnp.einsum("shgt,sthd->shgd", probs, values_view, preferred_element_type=jnp.float32)
    return (
        context
        + own_prob.astype(jnp.float32)[..., None] * own_value.astype(jnp.float32)[:, :, None, :]
    )


def local(
    hidden,
    cache_key,
    cache_value,
    lengths,
    owner,
    query_weight,
    key_weight,
    value_weight,
    out_weight,
):
    owner_rank = owner[0] % lax.axis_size("rep")
    features = lax.all_gather(hidden, "tp", axis=1, tiled=True)
    hidden_wide = features.astype(jnp.float32)
    normed = (
        hidden_wide
        * lax.rsqrt(jnp.mean(hidden_wide * hidden_wide, axis=-1, keepdims=True) + epsilon)
    ).astype(jnp.bfloat16)
    fresh_query, fresh_key, fresh_value, fresh_out = (
        from_root(query_weight, "rep", owner_rank),
        from_root(key_weight, "rep", owner_rank),
        from_root(value_weight, "rep", owner_rank),
        from_root(out_weight, "rep", owner_rank),
    )
    query_rows = fresh_query[0]
    key_rows = fresh_key[0]
    value_rows = fresh_value[0]
    out_cols = fresh_out[0]
    seqs = normed.shape[0]
    query_width = query_rows.shape[1]
    key_width = key_rows.shape[1]
    token_block = lax.all_to_all(normed, "fs", split_axis=1, concat_axis=0, tiled=True)
    joined = sent_and_summed(
        jnp.concatenate(
            [
                jnp.dot(token_block, query_rows, preferred_element_type=jnp.float32),
                jnp.dot(token_block, key_rows, preferred_element_type=jnp.float32),
                jnp.dot(token_block, value_rows, preferred_element_type=jnp.float32),
            ],
            axis=1,
        ),
        "fs",
        0,
    )
    query_proj = joined[:, :query_width]
    key_proj = joined[:, query_width : query_width + key_width]
    value_proj = joined[:, query_width + key_width :]
    q_heads = query_proj.shape[1] // DH
    kv_heads = key_proj.shape[1] // DH
    query_rot = rotate(query_proj.reshape(seqs, q_heads, DH), lengths).astype(jnp.bfloat16)
    query_rot = query_rot.reshape(seqs, kv_heads, q_heads // kv_heads, DH)
    key_new = rotate(key_proj.reshape(seqs, kv_heads, DH), lengths).astype(jnp.bfloat16)
    value_new = value_proj.astype(jnp.bfloat16).reshape(seqs, kv_heads, DH)
    context = attend(query_rot, key_new, value_new, cache_key, cache_value, lengths)
    context = context.astype(jnp.bfloat16).reshape(seqs, q_heads * DH)
    group_context = collect(context, "fs", 0)
    partial_out = jnp.dot(group_context, out_cols, preferred_element_type=jnp.float32)
    terms = lax.all_to_all(partial_out, "fs", split_axis=0, concat_axis=1, tiled=True)
    summed = sent_and_summed(terms, "tp", 1)
    mixed = (summed + hidden.astype(jnp.float32)).astype(jnp.bfloat16)
    return (
        mixed,
        key_new.reshape(seqs, kv_heads * DH),
        value_new.reshape(seqs, kv_heads * DH),
        fresh_query,
        fresh_key,
        fresh_value,
        fresh_out,
    )


def solution(mesh):
    return jax.shard_map(
        local,
        mesh=mesh,
        in_specs=(
            P(("rep", "fs"), "tp"),
            P(("rep", "fs"), None, "tp"),
            P(("rep", "fs"), None, "tp"),
            P(("rep", "fs")),
            P(),
            P("rep", "fs", "tp"),
            P("rep", "fs", "tp"),
            P("rep", "fs", "tp"),
            P("rep", "tp", "fs"),
        ),
        out_specs=(
            P(("rep", "fs"), "tp"),
            P(("rep", "fs"), "tp"),
            P(("rep", "fs"), "tp"),
            P("rep", "fs", "tp"),
            P("rep", "fs", "tp"),
            P("rep", "fs", "tp"),
            P("rep", "tp", "fs"),
        ),
        check_vma=False,
    )
```

profile of v0, /device:TPU:1, one launch (start us, length us, event | category | flops | bytes accessed | tf_op | source)
XLA Modules:
  0.0 207.0 jit_solution(11398649867773513769)
XLA Ops:
  8.0 1.5 broadcast_select_fusion
  9.5 0.9 copy-done.2
  10.3 1.5 broadcast_select_fusion.1
  11.9 1.0 broadcast_select_fusion.2
  13.0 0.7 copy-done.9
  13.6 23.1 %all_gather.3 = bf16[2,8192]{1,0:T(2,128)(2,1)S(1)} all-gather(bf16[2,1024]{1,0:T(2,128)(2,1)S(1)} %copy-done.9), channel_id=1, replica_groups=mesh['rep'=8,'tp'=8,'fs'=4] {'tp'}, dimensions={1}, use_global_device_ids=true | all-gather | bytes 36864 | tf_op jit(solution)/shard_map/all_gather | solution.py:103
  36.9 0.7 fusion.11
  37.6 10.9 %all-to-all-start = ((bf16[2,4,2048]{2,0,1:T(2,128)(2,1)}), bf16[2,4,2048]{2,0,1:T(2,128)(2,1)S(1)}, u32[]{:S(2)}, u32[]{:S(2)}) async-start(bf16[2,4,2048]{2,0,1:T(2,128)(2,1)} %bitcast), calls=%async_computation | async-start | bytes 65536 | tf_op jit(solution)/shard_map/all_to_all | solution.py:122
  48.7 5.2 %all-to-all-done = bf16[2,4,2048]{2,0,1:T(2,128)(2,1)S(1)} async-done(((bf16[2,4,2048]{2,0,1:T(2,128)(2,1)}), bf16[2,4,2048]{2,0,1:T(2,128)(2,1)S(1)}, u32[]{:S(2)}, u32[]{:S(2)}) %all-to-all-start) | async-done | bytes 32800 | tf_op jit(solution)/shard_map/all_to_all | solution.py:122
  53.9 93.1 %all-reduce.3.cloned.1.call-done = (bf16[1,2048,128]{2,1,0:T(8,128)(2,1)}, bf16[1,2048,128]{2,1,0:T(8,128)(2,1)}, bf16[1,2048,512]{2,1,0:T(8,128)(2,1)}, bf16[1,512,2048]{2,1,0:T(8,128)(2,1)}) async-done(((bf16[1,2048,128]{2,1,0:T(8,128)(2,1)}, bf16[1,2048,128]{2,1,0:T(8,128)(2,1)}, bf16[1,2048,512]{2,1,0:T(8,128)(2,1)}, bf16[1,512,2048]{2,1,0:T(8,128)(2,1)}), (bf16[1,2048,128]{2,1,0:T(8,128)(2,1)}, ...) | async-done | bytes 5242896 | tf_op jit(solution)/shard_map/psum | solution.py:13
  147.0 2.0 fusion.2
  149.5 0.6 reshape.245
  150.1 4.8 %all-to-all-start.1 = ((f32[4,2,768]{2,1,0:T(2,128)}), f32[4,2,768]{2,1,0:T(2,128)S(1)}, u32[]{:S(2)}, u32[]{:S(2)}) async-start(f32[4,2,768]{2,1,0:T(2,128)} %reshape.245), calls=%async_computation.1 | async-start | bytes 49152 | tf_op jit(solution)/shard_map/all_to_all | solution.py:24
  155.0 4.5 %all-to-all-done.1 = f32[4,2,768]{2,1,0:T(2,128)S(1)} async-done(((f32[4,2,768]{2,1,0:T(2,128)}), f32[4,2,768]{2,1,0:T(2,128)S(1)}, u32[]{:S(2)}, u32[]{:S(2)}) %all-to-all-start.1) | async-done | bytes 24608 | tf_op jit(solution)/shard_map/all_to_all | solution.py:24
  161.3 1.5 fusion.5
  162.9 7.7 %all_to_all.47 = bf16[4,2,512]{2,1,0:T(2,128)(2,1)S(1)} all-to-all(bf16[4,2,512]{2,1,0:T(2,128)(2,1)S(1)} %broadcast_in_dim.52), channel_id=1, replica_groups=mesh['rep'=8,'tp'=8,'fs'=4] {'fs'}, dimensions={0} | all-to-all | bytes 16384 | tf_op jit(solution)/shard_map/all_to_all | solution.py:30
  171.0 8.5 %all_to_all.48 = f32[4,2,2048]{2,1,0:T(2,128)} all-to-all(f32[4,2,2048]{2,1,0:T(2,128)S(1)} %fusion), channel_id=1, replica_groups=mesh['rep'=8,'tp'=8,'fs'=4] {'fs'}, dimensions={0} | all-to-all | bytes 131072 | tf_op jit(solution)/shard_map/all_to_all | solution.py:148
  179.5 6.7 %all-to-all-start.4 = ((f32[8,2,1024]{2,1,0:T(2,128)}), f32[8,2,1024]{2,1,0:T(2,128)S(1)}, u32[]{:S(2)}, u32[]{:S(2)}) async-start(f32[8,2,1024]{2,1,0:T(2,128)} %bitcast.16), calls=%async_computation.4 | async-start | bytes 131072 | tf_op jit(solution)/shard_map/all_to_all | solution.py:24
  186.8 6.6 %all-to-all-done.4 = f32[8,2,1024]{2,1,0:T(2,128)S(1)} async-done(((f32[8,2,1024]{2,1,0:T(2,128)}), f32[8,2,1024]{2,1,0:T(2,128)S(1)}, u32[]{:S(2)}, u32[]{:S(2)}) %all-to-all-start.4) | async-done | bytes 65568 | tf_op jit(solution)/shard_map/all_to_all | solution.py:24
  193.5 0.6 add_convert_fusion
  194.1 3.1 %copy.34 = bf16[1,2048,512]{2,1,0:T(8,128)(2,1)} copy(bf16[1,2048,512]{2,1,0:T(8,128)(2,1)} %get-tuple-element.28) | data formatting | bytes 4194304
  197.2 0.8 copy.35
  198.0 0.8 copy.36
  198.8 1.3 copy.37
  (50 shorter events, 3.8 us)
Async XLA Ops:
  7.2 153.4 %copy-start = (bf16[2,2048,128]{2,1,0:T(8,128)(2,1)S(1)}, bf16[2,2048,128]{2,1,0:T(8,128)(2,1)}, u32[]{:S(2)}) copy-start(bf16[2,2048,128]{2,1,0:T(8,128)(2,1)} %param.10) | copy-start | bytes 3145732
  7.2 139.8 %all-reduce.3.cloned.1.call-start = ((), (), s32[]{:S(2)}) async-start(), calls=%async_computation.5 | async-start | bytes 10485760 | tf_op jit(solution)/shard_map/psum | solution.py:13
  8.0 2.3 %copy-start.2 = (bf16[1,2048,512]{2,1,0:T(8,128)(2,1)S(1)}, bf16[1,2048,512]{2,1,0:T(8,128)(2,1)}, u32[]{:S(2)}) copy-start(bf16[1,2048,512]{2,1,0:T(8,128)(2,1)} %param.14) | copy-start | bytes 6291460
  10.3 1.5 copy-start.7
  10.3 1.6 copy-start.8
  12.9 0.7 copy-start.9
  12.9 35.6 %copy-start.10 = (s32[2]{0:T(128)S(1)}, s32[2]{0:T(128)}, u32[]{:S(2)}) copy-start(s32[2]{0:T(128)} %param.12) | copy-start | bytes 28
  37.6 16.2 %all-to-all-start = ((bf16[2,4,2048]{2,0,1:T(2,128)(2,1)}), bf16[2,4,2048]{2,0,1:T(2,128)(2,1)S(1)}, u32[]{:S(2)}, u32[]{:S(2)}) async-start(bf16[2,4,2048]{2,0,1:T(2,128)(2,1)} %bitcast), calls=%async_computation | async-start | bytes 65536 | tf_op jit(solution)/shard_map/all_to_all | solution.py:122
  147.0 2.1 copy-start.5
  147.0 2.2 %copy-start.3 = (bf16[1,2048,128]{2,1,0:T(8,128)(2,1)S(1)}, bf16[1,2048,128]{2,1,0:T(8,128)(2,1)}, u32[]{:S(2)}) copy-start(bf16[1,2048,128]{2,1,0:T(8,128)(2,1)} %get-tuple-element.30) | copy-start | bytes 1572868
  149.1 21.5 %copy-start.1 = (bf16[1,512,2048]{2,1,0:T(8,128)(2,1)S(1)}, bf16[1,512,2048]{2,1,0:T(8,128)(2,1)}, u32[]{:S(2)}) copy-start(bf16[1,512,2048]{2,1,0:T(8,128)(2,1)} %get-tuple-element.31) | copy-start | bytes 6291460
  150.1 9.4 %all-to-all-start.1 = ((f32[4,2,768]{2,1,0:T(2,128)}), f32[4,2,768]{2,1,0:T(2,128)S(1)}, u32[]{:S(2)}, u32[]{:S(2)}) async-start(f32[4,2,768]{2,1,0:T(2,128)} %reshape.245), calls=%async_computation.1 | async-start | bytes 49152 | tf_op jit(solution)/shard_map/all_to_all | solution.py:24
  179.5 14.0 %all-to-all-start.4 = ((f32[8,2,1024]{2,1,0:T(2,128)}), f32[8,2,1024]{2,1,0:T(2,128)S(1)}, u32[]{:S(2)}, u32[]{:S(2)}) async-start(f32[8,2,1024]{2,1,0:T(2,128)} %bitcast.16), calls=%async_computation.4 | async-start | bytes 131072 | tf_op jit(solution)/shard_map/all_to_all | solution.py:24
  194.1 3.1 %copy-start.6 = (bf16[1,2048,128]{2,1,0:T(8,128)(2,1)S(1)}, bf16[1,2048,128]{2,1,0:T(8,128)(2,1)}, u32[]{:S(2)}) copy-start(bf16[1,2048,128]{2,1,0:T(8,128)(2,1)} %get-tuple-element.29) | copy-start | bytes 1572868
  194.1 3.9 %copy-start.4 = (bf16[1,2048,128]{2,1,0:T(8,128)(2,1)S(1)}, bf16[1,2048,128]{2,1,0:T(8,128)(2,1)}, u32[]{:S(2)}) copy-start(bf16[1,2048,128]{2,1,0:T(8,128)(2,1)} %get-tuple-element.30) | copy-start | bytes 1572868
Sparse Core Ops, SparseCore 0:
  13.1 133.8 all-reduce.2
where the time goes:
time: 208 us; the launch traced here: 207 us
  waiting for transfers between devices  110 us (53%)
  blocking collectives  39.3 us (19%)
  starting transfers between devices  22.5 us (11%)
  between operations  14.9 us (7%)
  local copies, waits for them, and re-layouts  8.42 us (4%)
  other arithmetic  7.29 us (4%)
  matrix products  5.08 us (2%)
    psum x1, waiting for transfers between devices, from_root(): return lax.psum(jnp.where(mine, shard, jnp.zeros_like(shard)), axis)  93.1 us
    all_gather x1, blocking collectives, local(): features = lax.all_gather(hidden, 'tp', axis=1, tiled=True)  23.1 us
    all_to_all x2, starting transfers between devices, sent_and_summed(): parts = lax.all_to_all(cut_along(shard, dim, peers), axis, 0, 0, tiled=True)  11.5 us
    all_to_all x2, waiting for transfers between devices, sent_and_summed(): parts = lax.all_to_all(cut_along(shard, dim, peers), axis, 0, 0, tiled=True)  11.2 us
    all_to_all x1, starting transfers between devices, local(): lax.all_to_all(normed, 'fs', split_axis=1, concat_axis=0, tiled=True)  10.9 us
    all_to_all x1, blocking collectives, local(): lax.all_to_all(partial_out, 'fs', split_axis=0, concat_axis=1, tiled=True)  8.51 us
    unnamed x27, local copies, waits for them, and re-layouts  7.73 us
    all_to_all x1, blocking collectives, copy_for_each(): lax.all_to_all(jnp.broadcast_to(shard[None], (peers, *shard.shape)), axis...  7.7 us
  transfers between devices with their start and end apart: 4, of which 4 were waited for; matrix products, arithmetic and copies ran while one was open for 1% of the time, Pallas kernels for 0%

commit v1 on v0

--- a/solution.py
+++ b/solution.py
@@ -100,7 +100,8 @@
     out_weight,
 ):
     owner_rank = owner[0] % lax.axis_size("rep")
-    features = lax.all_gather(hidden, "tp", axis=1, tiled=True)
+    copies = jnp.concatenate([hidden] * lax.axis_size("tp"), axis=1)
+    features = lax.all_to_all(copies, "tp", 1, 1, tiled=True)
     hidden_wide = features.astype(jnp.float32)
     normed = (
         hidden_wide

time: 208 us -> 208 us (level)
  blocking collectives: 39.3 us -> 16.2 us
  waiting for transfers between devices: 110 us -> 123 us
  local copies, waits for them, and re-layouts: 8.42 us -> 13.8 us
  starting transfers between devices: 22.5 us -> 27 us
    all_gather x1 -> x0, blocking collectives: 23.1 us -> none  [local(): features = lax.all_gather(hidden, 'tp', axis=1, tiled=True)]
    all_to_all x0 -> x1, starting transfers between devices: none -> 9 us  [local(): features = lax.all_to_all(copies, 'tp', 1, 1, tiled=True)]
    psum x1, waiting for transfers between devices: 93.1 us -> 100 us  [from_root(): return lax.psum(jnp.where(mine, shard, jnp.zeros_like(shard)), axis)]
    all_to_all x0 -> x1, waiting for transfers between devices: none -> 6.79 us  [local(): features = lax.all_to_all(copies, 'tp', 1, 1, tiled=True)]
    all_to_all x1, starting transfers between devices: 10.9 us -> 6.39 us  [local(): lax.all_to_all(normed, 'fs', split_axis=1, concat_axis=0, tiled=True)]
    unnamed x27 -> x34, local copies, waits for them, and re-layouts: 7.73 us -> 11.9 us
  transfers between devices with their start and end apart: 4 -> 5, of which waited for: 4 -> 5; matrix products, arithmetic and copies ran while one was open for 1% -> 3% of each run, Pallas kernels for 0% -> 0%
where the time goes in v1:
time: 208 us; the launch traced here: 207 us
  waiting for transfers between devices  123 us (59%)
  starting transfers between devices  27 us (13%)
  blocking collectives  16.2 us (8%)
  between operations  14.9 us (7%)
  local copies, waits for them, and re-layouts  13.8 us (7%)
  other arithmetic  6.61 us (3%)
  matrix products  5.08 us (2%)
    psum x1, waiting for transfers between devices, from_root(): return lax.psum(jnp.where(mine, shard, jnp.zeros_like(shard)), axis)  100 us
    unnamed x34, local copies, waits for them, and re-layouts  11.9 us
    all_to_all x2, starting transfers between devices, sent_and_summed(): parts = lax.all_to_all(cut_along(shard, dim, peers), axis, 0, 0, tiled=True)  11.5 us
    all_to_all x2, waiting for transfers between devices, sent_and_summed(): parts = lax.all_to_all(cut_along(shard, dim, peers), axis, 0, 0, tiled=True)  11.2 us
    all_to_all x1, starting transfers between devices, local(): features = lax.all_to_all(copies, 'tp', 1, 1, tiled=True)  9 us
    all_to_all x1, blocking collectives, local(): lax.all_to_all(partial_out, 'fs', split_axis=0, concat_axis=1, tiled=True)  8.52 us
    all_to_all x1, blocking collectives, copy_for_each(): lax.all_to_all(jnp.broadcast_to(shard[None], (peers, *shard.shape)), axis...  7.7 us
    all_to_all x1, waiting for transfers between devices, local(): features = lax.all_to_all(copies, 'tp', 1, 1, tiled=True)  6.79 us
  transfers between devices with their start and end apart: 5, of which 5 were waited for; matrix products, arithmetic and copies ran while one was open for 3% of the time, Pallas kernels for 0%

profile of v1, /device:TPU:1, one launch (start us, length us, event | category | flops | bytes accessed | tf_op | source)
XLA Modules:
  0.0 207.0 jit_solution(6164412384185820031)
XLA Ops:
  8.0 1.5 broadcast_select_fusion
  9.5 0.9 copy-done.2
  10.3 1.5 broadcast_select_fusion.1
  11.9 1.0 broadcast_select_fusion.2
  13.0 0.7 copy-done.9
  18.4 9.0 %all-to-all-start = ((bf16[2,8,1024]{2,0,1:T(2,128)(2,1)}), bf16[2,8,1024]{2,0,1:T(2,128)(2,1)S(1)}, u32[]{:S(2)}, u32[]{:S(2)}) async-start(bf16[2,8,1024]{2,0,1:T(2,128)(2,1)} %bitcast), calls=%async_computation | async-start | bytes 65536 | tf_op jit(solution)/shard_map/all_to_all | solution.py:104
  27.5 6.8 %all-to-all-done = bf16[2,8,1024]{2,0,1:T(2,128)(2,1)S(1)} async-done(((bf16[2,8,1024]{2,0,1:T(2,128)(2,1)}), bf16[2,8,1024]{2,0,1:T(2,128)(2,1)S(1)}, u32[]{:S(2)}, u32[]{:S(2)}) %all-to-all-start) | async-done | bytes 32800 | tf_op jit(solution)/shard_map/all_to_all | solution.py:104
  34.5 0.6 copy.22
  35.2 6.4 %all-to-all-start.1 = ((bf16[2,4,2048]{2,0,1:T(2,128)(2,1)}), bf16[2,4,2048]{2,0,1:T(2,128)(2,1)S(1)}, u32[]{:S(2)}, u32[]{:S(2)}) async-start(bf16[2,4,2048]{2,0,1:T(2,128)(2,1)} %copy.22), calls=%async_computation.1 | async-start | bytes 65536 | tf_op jit(solution)/shard_map/all_to_all | solution.py:123
  41.6 5.3 %all-to-all-done.1 = bf16[2,4,2048]{2,0,1:T(2,128)(2,1)S(1)} async-done(((bf16[2,4,2048]{2,0,1:T(2,128)(2,1)}), bf16[2,4,2048]{2,0,1:T(2,128)(2,1)S(1)}, u32[]{:S(2)}, u32[]{:S(2)}) %all-to-all-start.1) | async-done | bytes 32800 | tf_op jit(solution)/shard_map/all_to_all | solution.py:123
  46.8 100.2 %all-reduce.3.cloned.1.call-done = (bf16[1,2048,128]{2,1,0:T(8,128)(2,1)}, bf16[1,2048,128]{2,1,0:T(8,128)(2,1)}, bf16[1,2048,512]{2,1,0:T(8,128)(2,1)}, bf16[1,512,2048]{2,1,0:T(8,128)(2,1)}) async-done(((bf16[1,2048,128]{2,1,0:T(8,128)(2,1)}, bf16[1,2048,128]{2,1,0:T(8,128)(2,1)}, bf16[1,2048,512]{2,1,0:T(8,128)(2,1)}, bf16[1,512,2048]{2,1,0:T(8,128)(2,1)}), (bf16[1,2048,128]{2,1,0:T(8,128)(2,1)}, ...) | async-done | bytes 5242896 | tf_op jit(solution)/shard_map/psum | solution.py:13
  147.0 2.0 fusion.2
  149.5 0.6 reshape.255
  150.1 4.8 %all-to-all-start.2 = ((f32[4,2,768]{2,1,0:T(2,128)}), f32[4,2,768]{2,1,0:T(2,128)S(1)}, u32[]{:S(2)}, u32[]{:S(2)}) async-start(f32[4,2,768]{2,1,0:T(2,128)} %reshape.255), calls=%async_computation.2 | async-start | bytes 49152 | tf_op jit(solution)/shard_map/all_to_all | solution.py:24
  155.0 4.5 %all-to-all-done.2 = f32[4,2,768]{2,1,0:T(2,128)S(1)} async-done(((f32[4,2,768]{2,1,0:T(2,128)}), f32[4,2,768]{2,1,0:T(2,128)S(1)}, u32[]{:S(2)}, u32[]{:S(2)}) %all-to-all-start.2) | async-done | bytes 24608 | tf_op jit(solution)/shard_map/all_to_all | solution.py:24
  161.3 1.5 fusion.5
  162.9 7.7 %all_to_all.53 = bf16[4,2,512]{2,1,0:T(2,128)(2,1)S(1)} all-to-all(bf16[4,2,512]{2,1,0:T(2,128)(2,1)S(1)} %broadcast_in_dim.52), channel_id=1, replica_groups=mesh['rep'=8,'tp'=8,'fs'=4] {'fs'}, dimensions={0} | all-to-all | bytes 16384 | tf_op jit(solution)/shard_map/all_to_all | solution.py:30
  171.0 8.5 %all_to_all.54 = f32[4,2,2048]{2,1,0:T(2,128)} all-to-all(f32[4,2,2048]{2,1,0:T(2,128)S(1)} %fusion), channel_id=1, replica_groups=mesh['rep'=8,'tp'=8,'fs'=4] {'fs'}, dimensions={0} | all-to-all | bytes 131072 | tf_op jit(solution)/shard_map/all_to_all | solution.py:149
  179.5 6.7 %all-to-all-start.5 = ((f32[8,2,1024]{2,1,0:T(2,128)}), f32[8,2,1024]{2,1,0:T(2,128)S(1)}, u32[]{:S(2)}, u32[]{:S(2)}) async-start(f32[8,2,1024]{2,1,0:T(2,128)} %bitcast.16), calls=%async_computation.5 | async-start | bytes 131072 | tf_op jit(solution)/shard_map/all_to_all | solution.py:24
  186.8 6.6 %all-to-all-done.5 = f32[8,2,1024]{2,1,0:T(2,128)S(1)} async-done(((f32[8,2,1024]{2,1,0:T(2,128)}), f32[8,2,1024]{2,1,0:T(2,128)S(1)}, u32[]{:S(2)}, u32[]{:S(2)}) %all-to-all-start.5) | async-done | bytes 65568 | tf_op jit(solution)/shard_map/all_to_all | solution.py:24
  194.1 3.1 %copy.49 = bf16[1,2048,512]{2,1,0:T(8,128)(2,1)} copy(bf16[1,2048,512]{2,1,0:T(8,128)(2,1)} %get-tuple-element.28) | data formatting | bytes 4194304
  197.2 0.8 copy.50
  198.0 0.8 copy.51
  198.8 1.3 copy.52
  (62 shorter events, 9.2 us)
Async XLA Ops:
  7.2 153.4 %copy-start = (bf16[2,2048,128]{2,1,0:T(8,128)(2,1)S(1)}, bf16[2,2048,128]{2,1,0:T(8,128)(2,1)}, u32[]{:S(2)}) copy-start(bf16[2,2048,128]{2,1,0:T(8,128)(2,1)} %param.10) | copy-start | bytes 3145732
  7.2 139.8 %all-reduce.3.cloned.1.call-start = ((), (), s32[]{:S(2)}) async-start(), calls=%async_computation.6 | async-start | bytes 10485760 | tf_op jit(solution)/shard_map/psum | solution.py:13
  8.0 2.3 %copy-start.2 = (bf16[1,2048,512]{2,1,0:T(8,128)(2,1)S(1)}, bf16[1,2048,512]{2,1,0:T(8,128)(2,1)}, u32[]{:S(2)}) copy-start(bf16[1,2048,512]{2,1,0:T(8,128)(2,1)} %param.14) | copy-start | bytes 6291460
  10.3 1.5 copy-start.7
  10.3 1.6 copy-start.8
  12.9 0.7 copy-start.9
  12.9 14.4 %copy-start.10 = (s32[2]{0:T(128)S(1)}, s32[2]{0:T(128)}, u32[]{:S(2)}) copy-start(s32[2]{0:T(128)} %param.12) | copy-start | bytes 28
  18.4 15.9 %all-to-all-start = ((bf16[2,8,1024]{2,0,1:T(2,128)(2,1)}), bf16[2,8,1024]{2,0,1:T(2,128)(2,1)S(1)}, u32[]{:S(2)}, u32[]{:S(2)}) async-start(bf16[2,8,1024]{2,0,1:T(2,128)(2,1)} %bitcast), calls=%async_computation | async-start | bytes 65536 | tf_op jit(solution)/shard_map/all_to_all | solution.py:104
  35.2 11.7 %all-to-all-start.1 = ((bf16[2,4,2048]{2,0,1:T(2,128)(2,1)}), bf16[2,4,2048]{2,0,1:T(2,128)(2,1)S(1)}, u32[]{:S(2)}, u32[]{:S(2)}) async-start(bf16[2,4,2048]{2,0,1:T(2,128)(2,1)} %copy.22), calls=%async_computation.1 | async-start | bytes 65536 | tf_op jit(solution)/shard_map/all_to_all | solution.py:123
  147.0 2.1 copy-start.5
  147.0 2.2 %copy-start.3 = (bf16[1,2048,128]{2,1,0:T(8,128)(2,1)S(1)}, bf16[1,2048,128]{2,1,0:T(8,128)(2,1)}, u32[]{:S(2)}) copy-start(bf16[1,2048,128]{2,1,0:T(8,128)(2,1)} %get-tuple-element.30) | copy-start | bytes 1572868
  149.1 21.5 %copy-start.1 = (bf16[1,512,2048]{2,1,0:T(8,128)(2,1)S(1)}, bf16[1,512,2048]{2,1,0:T(8,128)(2,1)}, u32[]{:S(2)}) copy-start(bf16[1,512,2048]{2,1,0:T(8,128)(2,1)} %get-tuple-element.31) | copy-start | bytes 6291460
  150.1 9.4 %all-to-all-start.2 = ((f32[4,2,768]{2,1,0:T(2,128)}), f32[4,2,768]{2,1,0:T(2,128)S(1)}, u32[]{:S(2)}, u32[]{:S(2)}) async-start(f32[4,2,768]{2,1,0:T(2,128)} %reshape.255), calls=%async_computation.2 | async-start | bytes 49152 | tf_op jit(solution)/shard_map/all_to_all | solution.py:24
  179.5 14.0 %all-to-all-start.5 = ((f32[8,2,1024]{2,1,0:T(2,128)}), f32[8,2,1024]{2,1,0:T(2,128)S(1)}, u32[]{:S(2)}, u32[]{:S(2)}) async-start(f32[8,2,1024]{2,1,0:T(2,128)} %bitcast.16), calls=%async_computation.5 | async-start | bytes 131072 | tf_op jit(solution)/shard_map/all_to_all | solution.py:24
  194.1 3.1 %copy-start.6 = (bf16[1,2048,128]{2,1,0:T(8,128)(2,1)S(1)}, bf16[1,2048,128]{2,1,0:T(8,128)(2,1)}, u32[]{:S(2)}) copy-start(bf16[1,2048,128]{2,1,0:T(8,128)(2,1)} %get-tuple-element.29) | copy-start | bytes 1572868
  194.1 3.9 %copy-start.4 = (bf16[1,2048,128]{2,1,0:T(8,128)(2,1)S(1)}, bf16[1,2048,128]{2,1,0:T(8,128)(2,1)}, u32[]{:S(2)}) copy-start(bf16[1,2048,128]{2,1,0:T(8,128)(2,1)} %get-tuple-element.30) | copy-start | bytes 1572868
Sparse Core Ops, SparseCore 0:
  13.1 133.8 all-reduce.2
